TPU v7x, 32 devices: a whole 2x2x4 slice. The times are simulated.
32 devices in a mesh: ckpt: 2 (over y), row: 4 (over z), col: 4 (over x, core).
Axes of the slice: x: 2, y: 2, z: 4, core: 2. Of those that a mesh axis runs over, the one named last changes fastest.
Arguments:
- grad_slab: bfloat16 [768, 27648], P(('ckpt', 'col'), 'row'), parts along dimension 0, may hold values from -6 to 6
- eigenbasis: bfloat16 [55296, 14336], P(('ckpt', 'row'), 'col'), parts along dimension 0, may hold values from -0.0546875 to 0.0546875
- eigenvalues: bfloat16 [768, 14336], P('ckpt', 'col'), parts along dimension 0, may hold values from 0.049804688 to 5
Outputs:
- preconditioned: bfloat16 [768, 27648], P(('ckpt', 'col'), 'row'), parts along dimension 0
There are 2 independent parts, one for each index of `ckpt`. A program takes and returns all parts, laid end to end along the dimension named above; each array names one. Nothing has to cross between parts.
All inputs are finite; a program needn't handle non-finite values.
Results may differ from a plain program's by a relative error of at most 0.0046.
Values may be sent and summed in bfloat16 or wider, within the bound.
No kernel may reach another device: no remote copies, remote signals or barrier semaphores. Data moves between devices by JAX's collectives and lax.ppermute only.
A program may use at most 128 MiB of HBM per device.

v0:
```python
import jax
import jax.numpy as jnp
from jax import lax
from jax.sharding import PartitionSpec as P

DAMPING = 0.1


def on_device(grad_slab, eigenbasis, eigenvalues):
    rotated_part = jnp.dot(
        lax.all_gather(grad_slab, "col", axis=0, tiled=True),
        eigenbasis,
        preferred_element_type=jnp.float32,
    )
    own_share = lax.psum_scatter(rotated_part, "row", scatter_dimension=1, tiled=True)
    share_width = own_share.shape[1]
    offset = lax.axis_index("row") * share_width
    own_values = lax.dynamic_slice_in_dim(eigenvalues, offset, share_width, 1)
    scaled_share = (own_share / (own_values.astype(jnp.float32) + DAMPING)).astype(jnp.bfloat16)
    scaled = lax.all_gather(scaled_share, "row", axis=1, tiled=True)
    result = lax.psum_scatter(
        lax.dot_general(
            scaled, eigenbasis, (((1,), (1,)), ((), ())), preferred_element_type=jnp.float32
        ),
        "col",
        scatter_dimension=0,
        tiled=True,
    )
    return result.astype(jnp.bfloat16)


def solution(mesh):
    placed = (P(("ckpt", "col"), "row"), P(("ckpt", "row"), "col"), P("ckpt", "col"))
    return jax.shard_map(
        on_device, mesh=mesh, in_specs=placed, out_specs=P(("ckpt", "col"), "row"), check_vma=False
    )
```

profile of v0, /device:TPU:0, one launch (start us, length us, event | category | flops | bytes accessed | tf_op | source)
XLA Modules:
  0.0 360.5 jit_solution(17615250611233539251)
XLA Ops:
  6.5 0.0 all-gather.3.cloned.1.call-start
  6.5 0.7 all-gather.3.cloned.1.call-update
  7.3 0.0 reduce-scatter.3.cloned.1.call-start
  7.3 45.1 %all-gather.3.cloned.1.call-done = bf16[384,6912]{1,0:T(8,128)(2,1)} async-done(((bf16[96,6912]{1,0:T(8,128)(2,1)}), bf16[384,6912]{1,0:T(8,128)(2,1)}) %all-gather.3.cloned.1.call-update) | async-done | bytes 5308432 | tf_op jit(solution)/shard_map/all_gather | solution.py:11
  52.4 28.3 %fusion = f32[384,3584]{1,0:T(8,128)} fusion(bf16[384,6912]{1,0:T(8,128)(2,1)} %all-gather.3.cloned.1.call-done, bf16[6912,3584]{1,0:T(8,128)(2,1)} %param.4), kind=kOutput, calls=%fused_computation.1 | convolution fusion | flops 19025362944 | bytes 60358656 | tf_op jit(solution)/shard_map/dot_general | solution.py:10
  80.7 0.0 reduce-scatter.3.cloned.1.call-update
  80.8 0.0 all-gather.5.cloned.1.call-start
  80.8 98.1 %reduce-scatter.3.cloned.1.call-done = f32[384,896]{1,0:T(8,128)} async-done(((f32[384,3584]{1,0:T(8,128)}), f32[384,896]{1,0:T(8,128)}) %reduce-scatter.3.cloned.1.call-update) | async-done | bytes 1376272 | tf_op jit(solution)/shard_map/reduce_scatter | solution.py:15
  178.9 2.6 divide_convert_fusion
  181.5 0.0 all-gather.5.cloned.1.call-update
  181.5 0.0 reduce-scatter.5.cloned.1.call-start
  181.6 57.4 %all-gather.5.cloned.1.call-done = bf16[384,3584]{1,0:T(8,128)(2,1)} async-done(((bf16[384,896]{1,0:T(8,128)(2,1)}), bf16[384,3584]{1,0:T(8,128)(2,1)}) %all-gather.5.cloned.1.call-update) | async-done | bytes 2752528 | tf_op jit(solution)/shard_map/all_gather | solution.py:20
  239.0 28.0 %fusion.1 = f32[384,6912]{1,0:T(8,128)} fusion(bf16[384,3584]{1,0:T(8,128)(2,1)} %all-gather.5.cloned.1.call-done, bf16[6912,3584]{1,0:T(8,128)(2,1)} %param.4), kind=kOutput, calls=%fused_computation.2 | convolution fusion | flops 19025362944 | bytes 62914560 | tf_op jit(solution)/shard_map/dot_general | solution.py:22
  267.0 0.0 reduce-scatter.5.cloned.1.call-update
  267.0 84.0 %reduce-scatter.5.cloned.1.call-done = f32[96,6912]{1,0:T(8,128)} async-done(((f32[384,6912]{1,0:T(8,128)}), f32[96,6912]{1,0:T(8,128)}) %reduce-scatter.5.cloned.1.call-update) | async-done | bytes 2654224 | tf_op jit(solution)/shard_map/reduce_scatter | solution.py:21
  351.0 2.9 convert_element_type.11
Async XLA Ops:
  6.5 45.9 %all-gather.3.cloned.1.call-start = ((), (), s32[]{:S(2)}) async-start(), calls=%async_computation.2 | async-start | bytes 6635520 | tf_op jit(solution)/shard_map/all_gather | solution.py:11
  7.3 171.7 %reduce-scatter.3.cloned.1.call-start = ((), (), s32[]{:S(2)}) async-start(), calls=%async_computation.3 | async-start | bytes 6881280 | tf_op jit(solution)/shard_map/reduce_scatter | solution.py:15
  80.8 158.2 %all-gather.5.cloned.1.call-start = ((), (), s32[]{:S(2)}) async-start(), calls=%async_computation.4 | async-start | bytes 3440640 | tf_op jit(solution)/shard_map/all_gather | solution.py:20
  181.5 169.5 %reduce-scatter.5.cloned.1.call-start = ((), (), s32[]{:S(2)}) async-start(), calls=%async_computation.5 | async-start | bytes 13271040 | tf_op jit(solution)/shard_map/reduce_scatter | solution.py:21
Sparse Core Ops, SparseCore 0:
  8.9 43.4 all-gather.2
  80.9 98.0 reduce-scatter.2
  181.7 57.2 all-gather.4
  267.1 83.8 reduce-scatter.4
where the time goes:
time: 361 us; the launch traced here: 360 us
  waiting for transfers between devices  285 us (79%)
  matrix products  56.3 us (16%)
  between operations  13.1 us (4%)
  other arithmetic  5.52 us (2%)
    reduce_scatter x1, waiting for transfers between devices, on_device(): lax.psum_scatter(rotated_part, 'row', scatter_dimension=1, tiled=True)  98.1 us
    reduce_scatter x1, waiting for transfers between devices, on_device(): lax.psum_scatter(lax.dot_general(scaled, eigenbasis, (((1,), (1,)), ((),...  84 us
    all_gather x1, waiting for transfers between devices, on_device(): scaled = lax.all_gather(scaled_share, 'row', axis=1, tiled=True)  57.4 us
    all_gather x1, waiting for transfers between devices, on_device(): lax.all_gather(grad_slab, 'col', axis=0, tiled=True)  45.1 us
    dot_general x1, matrix products, on_device(): jnp.dot(lax.all_gather(grad_slab, 'col', axis=0, tiled=True), eigenbasis,...  28.3 us
    dot_general x1, matrix products, on_device(): lax.dot_general(scaled, eigenbasis, (((1,), (1,)), ((), ())), preferred_e...  28 us
  transfers between devices with their start and end apart: 4, of which 4 were waited for; matrix products, arithmetic and copies ran while one was open for 0% of the time, Pallas kernels for 0%

commit v1 on v0

--- a/solution.py
+++ b/solution.py
@@ -8,7 +8,9 @@
 
 def on_device(grad_slab, eigenbasis, eigenvalues):
     rotated_part = jnp.dot(
-        lax.all_gather(grad_slab, "col", axis=0, tiled=True),
+        jnp.concatenate(
+            lax.all_to_all(jnp.stack([grad_slab] * lax.axis_size("col")), "col", 0, 0), axis=0
+        ),
         eigenbasis,
         preferred_element_type=jnp.float32,
     )

time: 361 us -> 379 us (1.050)
  blocking collectives: 0 us -> 64.1 us
  waiting for transfers between devices: 285 us -> 240 us
    all_to_all x0 -> x1, blocking collectives: none -> 64.1 us  [on_device(): lax.all_to_all(jnp.stack([grad_slab] * lax.axis_size('col')), 'col', 0, 0)]
    all_gather x1 -> x0, waiting for transfers between devices: 45.1 us -> none  [on_device(): lax.all_gather(grad_slab, 'col', axis=0, tiled=True)]
  transfers between devices with their start and end apart: 4 -> 3, of which waited for: 4 -> 3; matrix products, arithmetic and copies ran while one was open for 0% -> 0% of each run, Pallas kernels for 0% -> 0%
where the time goes in v1:
time: 379 us
  waiting for transfers between devices  240 us (63%)
  blocking collectives  64.1 us (17%)
  matrix products  54.3 us (14%)
  between operations  13.1 us (3%)
  other arithmetic  5.52 us (1%)
    reduce_scatter x1, waiting for transfers between devices, on_device(): lax.psum_scatter(rotated_part, 'row', scatter_dimension=1, tiled=True)  98.5 us
    reduce_scatter x1, waiting for transfers between devices, on_device(): lax.psum_scatter(lax.dot_general(scaled, eigenbasis, (((1,), (1,)), ((),...  84 us
    all_to_all x1, blocking collectives, on_device(): lax.all_to_all(jnp.stack([grad_slab] * lax.axis_size('col')), 'col', 0, 0)  64.1 us
    all_gather x1, waiting for transfers between devices, on_device(): scaled = lax.all_gather(scaled_share, 'row', axis=1, tiled=True)  57.3 us
    dot_general x1, matrix products, on_device(): lax.dot_general(scaled, eigenbasis, (((1,), (1,)), ((), ())), preferred_e...  28.1 us
    dot_general x1, matrix products, on_device(): jnp.dot(jnp.concatenate(lax.all_to_all(jnp.stack([grad_slab] * lax.axis_s...  26.2 us
  transfers between devices with their start and end apart: 3, of which 3 were waited for; matrix products, arithmetic and copies ran while one was open for 0% of the time, Pallas kernels for 0%

profile of v1, /device:TPU:0, one launch (start us, length us, event | category | flops | bytes accessed | tf_op | source)
XLA Modules:
  0.0 378.7 jit_solution(14741459584438241539)
XLA Ops:
  6.5 0.0 reduce-scatter.3.cloned.1.call-start
  6.5 1.7 stack.2
  8.2 64.1 %all_to_all.5 = bf16[4,96,6912]{2,1,0:T(8,128)(2,1)S(1)} all-to-all(bf16[4,96,6912]{2,1,0:T(8,128)(2,1)S(1)} %stack.2), channel_id=1, replica_groups=mesh['ckpt'=2,'row'=4,'col'=4] {'col'}, dimensions={0} | all-to-all | bytes 10616832 | tf_op jit(solution)/shard_map/all_to_all | solution.py:12
  72.3 26.2 %fusion = f32[384,3584]{1,0:T(8,128)} fusion(bf16[384,6912]{1,0:T(8,128)(2,1)S(1)} %bitcast.5, bf16[6912,3584]{1,0:T(8,128)(2,1)} %param.4), kind=kOutput, calls=%fused_computation.1 | convolution fusion | flops 19025362944 | bytes 60358656 | tf_op jit(solution)/shard_map/dot_general | solution.py:10
  98.5 0.0 reduce-scatter.3.cloned.1.call-update
  98.6 0.0 all-gather.2.cloned.1.call-start
  98.6 98.5 %reduce-scatter.3.cloned.1.call-done = f32[384,896]{1,0:T(8,128)} async-done(((f32[384,3584]{1,0:T(8,128)}), f32[384,896]{1,0:T(8,128)}) %reduce-scatter.3.cloned.1.call-update) | async-done | bytes 1376272 | tf_op jit(solution)/shard_map/reduce_scatter | solution.py:17
  197.1 2.6 divide_convert_fusion
  199.7 0.0 all-gather.2.cloned.1.call-update
  199.7 0.0 reduce-scatter.5.cloned.1.call-start
  199.8 57.3 %all-gather.2.cloned.1.call-done = bf16[384,3584]{1,0:T(8,128)(2,1)} async-done(((bf16[384,896]{1,0:T(8,128)(2,1)}), bf16[384,3584]{1,0:T(8,128)(2,1)}) %all-gather.2.cloned.1.call-update) | async-done | bytes 2752528 | tf_op jit(solution)/shard_map/all_gather | solution.py:22
  257.1 28.1 %fusion.1 = f32[384,6912]{1,0:T(8,128)} fusion(bf16[384,3584]{1,0:T(8,128)(2,1)} %all-gather.2.cloned.1.call-done, bf16[6912,3584]{1,0:T(8,128)(2,1)} %param.4), kind=kOutput, calls=%fused_computation.2 | convolution fusion | flops 19025362944 | bytes 62914560 | tf_op jit(solution)/shard_map/dot_general | solution.py:24
  285.2 0.0 reduce-scatter.5.cloned.1.call-update
  285.2 84.0 %reduce-scatter.5.cloned.1.call-done = f32[96,6912]{1,0:T(8,128)} async-done(((f32[384,6912]{1,0:T(8,128)}), f32[96,6912]{1,0:T(8,128)}) %reduce-scatter.5.cloned.1.call-update) | async-done | bytes 2654224 | tf_op jit(solution)/shard_map/reduce_scatter | solution.py:23
  369.2 2.9 convert_element_type.11
Async XLA Ops:
  6.5 190.6 %reduce-scatter.3.cloned.1.call-start = ((), (), s32[]{:S(2)}) async-start(), calls=%async_computation.3 | async-start | bytes 6881280 | tf_op jit(solution)/shard_map/reduce_scatter | solution.py:17
  98.6 158.5 %all-gather.2.cloned.1.call-start = ((), (), s32[]{:S(2)}) async-start(), calls=%async_computation.4 | async-start | bytes 3440640 | tf_op jit(solution)/shard_map/all_gather | solution.py:22
  199.7 169.5 %reduce-scatter.5.cloned.1.call-start = ((), (), s32[]{:S(2)}) async-start(), calls=%async_computation.5 | async-start | bytes 13271040 | tf_op jit(solution)/shard_map/reduce_scatter | solution.py:23
Sparse Core Ops, SparseCore 0:
  98.7 98.3 reduce-scatter.2
  199.8 57.2 all-gather.1
  285.3 83.8 reduce-scatter.4

commit v2 on v0

--- a/solution.py
+++ b/solution.py
@@ -4,6 +4,25 @@
 from jax.sharding import PartitionSpec as P
 
 DAMPING = 0.1
+
+
+def laid_out(tiles, dim):
+    shape = list(tiles.shape[1:])
+    shape[dim] *= tiles.shape[0]
+    return jnp.moveaxis(tiles, 0, dim).reshape(shape)
+
+
+def doubled(array, axis):
+    size, index = (lax.axis_size(axis), lax.axis_index(axis))
+    blocks, bit = (array[None], 1)
+    while bit < size:
+        partner_block = lax.ppermute(blocks, axis, [(i, i ^ bit) for i in range(size)])
+        low = index & bit == 0
+        blocks = jnp.concatenate(
+            [jnp.where(low, blocks, partner_block), jnp.where(low, partner_block, blocks)]
+        )
+        bit *= 2
+    return blocks
 
 
 def on_device(grad_slab, eigenbasis, eigenvalues):
@@ -17,7 +36,7 @@
     offset = lax.axis_index("row") * share_width
     own_values = lax.dynamic_slice_in_dim(eigenvalues, offset, share_width, 1)
     scaled_share = (own_share / (own_values.astype(jnp.float32) + DAMPING)).astype(jnp.bfloat16)
-    scaled = lax.all_gather(scaled_share, "row", axis=1, tiled=True)
+    scaled = laid_out(doubled(scaled_share, "row"), 1)
     result = lax.psum_scatter(
         lax.dot_general(
             scaled, eigenbasis, (((1,), (1,)), ((), ())), preferred_element_type=jnp.float32

time: 361 us -> 388 us (1.075)
  waiting for transfers between devices: 285 us -> 304 us
  starting transfers between devices: 0.13 us -> 4.54 us
    ppermute x0 -> x2, waiting for transfers between devices: none -> 74.6 us  [doubled(): lax.ppermute(blocks, axis, [(i, i ^ bit) for i in range(size)])]
    all_gather x1 -> x0, waiting for transfers between devices: 57.4 us -> none  [on_device(): scaled = lax.all_gather(scaled_share, 'row', axis=1, tiled=True)]
    ppermute x0 -> x2, starting transfers between devices: none -> 4.46 us  [doubled(): lax.ppermute(blocks, axis, [(i, i ^ bit) for i in range(size)])]
  transfers between devices with their start and end apart: 4 -> 5, of which waited for: 4 -> 5; matrix products, arithmetic and copies ran while one was open for 0% -> 0% of each run, Pallas kernels for 0% -> 0%
where the time goes in v2:
time: 388 us
  waiting for transfers between devices  304 us (78%)
  matrix products  56.5 us (15%)
  between operations  13.1 us (3%)
  other arithmetic  6.63 us (2%)
  starting transfers between devices  4.54 us (1%)
    reduce_scatter x1, waiting for transfers between devices, on_device(): lax.psum_scatter(rotated_part, 'row', scatter_dimension=1, tiled=True)  98.1 us
    reduce_scatter x1, waiting for transfers between devices, on_device(): lax.psum_scatter(lax.dot_general(scaled, eigenbasis, (((1,), (1,)), ((),...  85.5 us
    ppermute x2, waiting for transfers between devices, doubled(): lax.ppermute(blocks, axis, [(i, i ^ bit) for i in range(size)])  74.6 us
    all_gather x1, waiting for transfers between devices, on_device(): lax.all_gather(grad_slab, 'col', axis=0, tiled=True)  45.1 us
    dot_general x1, matrix products, on_device(): jnp.dot(lax.all_gather(grad_slab, 'col', axis=0, tiled=True), eigenbasis,...  28.3 us
    dot_general x1, matrix products, on_device(): lax.dot_general(scaled, eigenbasis, (((1,), (1,)), ((), ())), preferred_e...  28.1 us
  transfers between devices with their start and end apart: 5, of which 5 were waited for; matrix products, arithmetic and copies ran while one was open for 0% of the time, Pallas kernels for 0%

profile of v2, /device:TPU:0, one launch (start us, length us, event | category | flops | bytes accessed | tf_op | source)
XLA Modules:
  0.0 387.6 jit_solution(14045205044757180414)
XLA Ops:
  6.5 0.0 all-gather.2.cloned.1.call-start
  6.5 0.7 all-gather.2.cloned.1.call-update
  7.3 0.0 reduce-scatter.3.cloned.1.call-start
  7.3 45.1 %all-gather.2.cloned.1.call-done = bf16[384,6912]{1,0:T(8,128)(2,1)} async-done(((bf16[96,6912]{1,0:T(8,128)(2,1)}), bf16[384,6912]{1,0:T(8,128)(2,1)}) %all-gather.2.cloned.1.call-update) | async-done | bytes 5308432 | tf_op jit(solution)/shard_map/all_gather | solution.py:30
  52.4 28.3 %fusion.1 = f32[384,3584]{1,0:T(8,128)} fusion(bf16[384,6912]{1,0:T(8,128)(2,1)} %all-gather.2.cloned.1.call-done, bf16[6912,3584]{1,0:T(8,128)(2,1)} %param.4), kind=kOutput, calls=%fused_computation.8 | convolution fusion | flops 19025362944 | bytes 60358656 | tf_op jit(solution)/shard_map/dot_general | solution.py:29
  80.7 0.0 reduce-scatter.3.cloned.1.call-update
  80.8 0.0 reduce-scatter.5.cloned.1.call-start
  80.8 98.1 %reduce-scatter.3.cloned.1.call-done = f32[384,896]{1,0:T(8,128)} async-done(((f32[384,3584]{1,0:T(8,128)}), f32[384,896]{1,0:T(8,128)}) %reduce-scatter.3.cloned.1.call-update) | async-done | bytes 1376272 | tf_op jit(solution)/shard_map/reduce_scatter | solution.py:34
  178.9 1.7 fusion
  180.7 1.6 collective-permute-start
  182.2 15.7 %collective-permute-done = bf16[1,384,896]{2,1,0:T(8,128)(2,1)S(1)} collective-permute-done((bf16[1,384,896]{2,1,0:T(8,128)(2,1)S(1)}, bf16[1,384,896]{2,1,0:T(8,128)(2,1)S(1)}, u32[]{:S(2)}, u32[]{:S(2)}) %collective-permute-start) | collective-permute-done | bytes 688160 | tf_op jit(solution)/shard_map/ppermute | solution.py:19
  197.9 0.1 broadcast_select_fusion.3
  198.0 1.3 pad_maximum_fusion
  199.3 2.9 collective-permute-start.1
  202.2 59.0 %collective-permute-done.1 = bf16[2,384,896]{2,1,0:T(8,128)(2,1)S(1)} collective-permute-done((bf16[2,384,896]{2,1,0:T(8,128)(2,1)}, bf16[2,384,896]{2,1,0:T(8,128)(2,1)S(1)}, u32[]{:S(2)}, u32[]{:S(2)}) %collective-permute-start.1) | collective-permute-done | bytes 1376288 | tf_op jit(solution)/shard_map/ppermute | solution.py:19
  261.1 0.3 broadcast_select_fusion.1
  261.4 0.3 maximum_bitcast_fusion
  261.7 2.8 copy.4
  264.5 28.1 %fusion.2 = f32[384,6912]{1,0:T(8,128)} fusion(bf16[384,3584]{0,1:T(8,128)(2,1)} %bitcast.9, bf16[6912,3584]{1,0:T(8,128)(2,1)} %param.4), kind=kOutput, calls=%fused_computation.9 | convolution fusion | flops 19025362944 | bytes 62914560 | tf_op jit(solution)/shard_map/dot_general | solution.py:41
  292.6 0.0 reduce-scatter.5.cloned.1.call-update
  292.7 85.5 %reduce-scatter.5.cloned.1.call-done = f32[96,6912]{1,0:T(8,128)} async-done(((f32[384,6912]{1,0:T(8,128)}), f32[96,6912]{1,0:T(8,128)}) %reduce-scatter.5.cloned.1.call-update) | async-done | bytes 2654224 | tf_op jit(solution)/shard_map/reduce_scatter | solution.py:40
  378.1 2.9 convert_element_type.11
Async XLA Ops:
  6.5 45.9 %all-gather.2.cloned.1.call-start = ((), (), s32[]{:S(2)}) async-start(), calls=%async_computation.2 | async-start | bytes 6635520 | tf_op jit(solution)/shard_map/all_gather | solution.py:30
  7.3 171.7 %reduce-scatter.3.cloned.1.call-start = ((), (), s32[]{:S(2)}) async-start(), calls=%async_computation.3 | async-start | bytes 6881280 | tf_op jit(solution)/shard_map/reduce_scatter | solution.py:34
  80.8 297.4 %reduce-scatter.5.cloned.1.call-start = ((), (), s32[]{:S(2)}) async-start(), calls=%async_computation.4 | async-start | bytes 13271040 | tf_op jit(solution)/shard_map/reduce_scatter | solution.py:40
  180.7 17.2 %collective-permute-start = (bf16[1,384,896]{2,1,0:T(8,128)(2,1)S(1)}, bf16[1,384,896]{2,1,0:T(8,128)(2,1)S(1)}, u32[]{:S(2)}, u32[]{:S(2)}) collective-permute-start(bf16[1,384,896]{2,1,0:T(8,128)(2,1)S(1)} %fusion), channel_id=1, source_target_pairs={{0,4},{4,0},{8,12},{12,8},{1,5},{5,1},{9,13},{13,9},{2,6},{6,2},{1... | collective-permute-start | bytes 2064392 | tf_op jit(solution)/shard_map/ppermute | solution.py:19
  199.3 61.9 %collective-permute-start.1 = (bf16[2,384,896]{2,1,0:T(8,128)(2,1)}, bf16[2,384,896]{2,1,0:T(8,128)(2,1)S(1)}, u32[]{:S(2)}, u32[]{:S(2)}) collective-permute-start(bf16[2,384,896]{2,1,0:T(8,128)(2,1)} %pad_maximum_fusion), channel_id=1, source_target_pairs={{0,8},{4,12},{8,0},{12,4},{1,9},{5,13},{9,1},{13,5},{2,10},{6,14},... | collective-permute-start | bytes 4128776 | tf_op jit(solution)/shard_map/ppermute | solution.py:19
Sparse Core Ops, SparseCore 0:
  8.9 43.4 all-gather.1
  80.9 98.0 reduce-scatter.2
  292.8 85.3 reduce-scatter.4
